TPU v7x, 256 devices: a whole 4x4x8 slice. The times are simulated.
256 devices in a mesh: row: 16 (over z_lo, x), col: 16 (over z_hi, y, core).
Axes of the slice: x: 4, y: 4, z: 8 (z_hi: 2, z_lo: 4; z = z_hi * 4 + z_lo), core: 2. Of those that a mesh axis runs over, the one named last changes fastest.
Arguments:
- samples: float32 [32768, 512], P(('row', 'col')), may hold values from -8 to 8
- labels: int32 [32768, 256], P(('row', 'col')), may hold values from -1 to 1, as said below
Outputs:
- statistic: float32 [256], replicated
- proof: float32 [32768], P(('row', 'col'))
- p_value: float32 [], replicated
Inputs may be any that keep to these rules, and one draw needn't show every extreme that they name: `labels`: every column holds exactly 16384 entries +1 and 16384 entries -1.
All inputs are finite; a program needn't handle non-finite values.
Results may differ from a plain program's by a relative error of at most 0.0003.
Values sent between devices are 32-bit elements; how exact they have to be, the bound alone decides.
No kernel may reach another device: no remote copies, remote signals or barrier semaphores. Data moves between devices by JAX's collectives and lax.ppermute only.
A program may use at most 64 MiB of HBM per device.

v0:
```python
import functools
import math

import jax
import jax.numpy as jnp
from jax import lax
from jax.sharding import Mesh
from jax.sharding import PartitionSpec as P

ROW = ("row_0", "row_1")
COL = ("col_0", "col_1", "col_2")
ROW_COL = ("row_0", "row_1", "col_0", "col_1", "col_2")


def side_by_side(arrays, axis, dim, along):
    widths = [a.shape[along] for a in arrays]
    both = jnp.concatenate(arrays, axis=along)
    out = lax.all_gather(both, axis, axis=dim, tiled=True)
    return tuple(jnp.split(out, [sum(widths[:k]) for k in range(1, len(widths))], axis=along))


def cut_along(shard, dim, length):
    lengths = shard.shape
    tiles = shard.reshape(*lengths[:dim], length, lengths[dim] // length, *lengths[dim + 1 :])
    return jnp.moveaxis(tiles, dim, 0)


def summed_on_arrival(shard, axis, dim):
    length = lax.axis_size(axis)
    tiles = lax.all_to_all(cut_along(shard, dim, length), axis, 0, 0, tiled=True)
    return jnp.sum(tiles, axis=0)


def one_axis_at_a_time(shard, axes):
    return functools.reduce(lax.psum, axes, shard)


def tile_terms(xr, lr, gr, xc, lc, gc, width):
    norm_rows = jnp.sum(xr * xr, 1)
    norm_cols = jnp.sum(xc * xc, 1)
    dots = lax.dot_general(
        xr,
        xc,
        (((1,), (1,)), ((), ())),
        precision=lax.Precision.HIGHEST,
        preferred_element_type=jnp.float32,
    )
    dist = jnp.maximum(norm_rows[:, None] + norm_cols[None, :] - 2.0 * dots, 0.0)
    kern = jnp.where(gr[:, None] == gc[None, :], 0.0, jnp.exp(-dist / (2.0 * width)))
    proj = jnp.dot(kern, lc, precision=lax.Precision.HIGHEST, preferred_element_type=jnp.float32)
    return (proj[:, 0], jnp.sum(lr * proj, 0), jnp.sum(kern))


def rows_terms(row_x, row_l, row_ids, col_x, col_l, col_ids, width):
    block = row_x.shape[0]
    perms = row_l.shape[1]
    tile = math.gcd(block, 512)
    count = block // tile

    def one(args):
        xr, lr, gr = args
        return tile_terms(xr, lr, gr, col_x, col_l, col_ids, width)

    wit, quad, tot = lax.map(
        one,
        (
            row_x.reshape(count, tile, width),
            row_l.reshape(count, tile, perms),
            row_ids.reshape(count, tile),
        ),
    )
    return (wit.reshape(block), jnp.sum(quad, 0), jnp.sum(tot))


def shards(samples, labels):
    shard = samples.shape[0]
    width = samples.shape[1]
    n_row = lax.axis_size(ROW)
    n_col = lax.axis_size(COL)
    block = shard * n_col
    labs = labels.astype(jnp.float32)
    row_x, row_l = side_by_side((samples, labs), COL, 0, 1)
    row_ids = lax.axis_index(ROW) * block + jnp.arange(block, dtype=jnp.int32)
    col_base = lax.axis_index(COL) * shard
    col_x, col_l = side_by_side((samples, labs), ROW, 0, 1)
    positions = jnp.arange(shard * n_row, dtype=jnp.int32)
    col_ids = positions // shard * block + col_base + positions % shard
    wit, quad, total = rows_terms(row_x, row_l, row_ids, col_x, col_l, col_ids, width)
    all_rows = shard * n_row * n_col
    own_wit = summed_on_arrival(wit, COL, 0)
    proof = own_wit / jnp.sqrt(jnp.float32(all_rows))
    quad, total = (one_axis_at_a_time(quad, ROW_COL), one_axis_at_a_time(total, ROW_COL))
    half = all_rows / 2.0
    statistic = (
        total / (2.0 * half * (half - 1.0))
        + (2.0 * half - 1.0) / (2.0 * half * (half - 1.0)) * quad
    )
    p_value = jnp.mean(jax.nn.sigmoid(4.0 * (statistic[1:] - statistic[0])))
    return (statistic, proof, p_value)


def solution(mesh):
    torus = Mesh(mesh.devices.reshape(4, 4, 2, 4, 2), ("row_0", "row_1", "col_0", "col_1", "col_2"))
    return jax.shard_map(
        shards,
        mesh=torus,
        in_specs=(P(ROW_COL, None), P(ROW_COL, None)),
        out_specs=(P(), P(ROW_COL), P()),
        check_vma=False,
    )
```

profile of v0, /device:TPU:1, one launch (start us, length us, event | category | flops | bytes accessed | tf_op | source)
XLA Modules:
  0.0 347.3 jit_solution(409307274254476558)
XLA Ops:
  7.2 0.0 all-gather.5.cloned.1.call-start
  7.2 0.9 convert_element_type.3
  8.1 1.7 pad_maximum_fusion
  9.8 0.0 all-gather.5.cloned.1.call-update
  9.9 0.0 all-gather.3.cloned.1.call-start
  9.9 0.7 all-gather.3.cloned.1.call-update
  10.7 86.4 %all-gather.5.cloned.1.call-done = f32[2048,768]{1,0:T(8,128)} async-done(((f32[128,768]{1,0:T(8,128)}), f32[2048,768]{1,0:T(8,128)}) %all-gather.5.cloned.1.call-update) | async-done | bytes 6291472 | tf_op jit(solution)/shard_map/all_gather | solution.py:18
  97.0 4.5 %fusion.19 = (f32[2048,512]{1,0:T(8,128)}, f32[2048]{0:T(1024)S(1)}) fusion(f32[2048,768]{1,0:T(8,128)} %all-gather.5.cloned.1.call-done), kind=kLoop, calls=%fused_computation.34 | loop fusion | flops 2095104 | bytes 8396800 | tf_op jit(solution)/shard_map/split | solution.py:19
  101.5 97.4 %all-gather.3.cloned.1.call-done = f32[2048,768]{1,0:T(8,128)} async-done(((f32[128,768]{1,0:T(8,128)}), f32[2048,768]{1,0:T(8,128)}) %all-gather.3.cloned.1.call-update) | async-done | bytes 6291472 | tf_op jit(solution)/shard_map/all_gather | solution.py:18
  199.0 3.1 split.19
  202.0 4.7 %split.16 = f32[2048,512]{1,0:T(8,128)} slice(f32[2048,768]{1,0:T(8,128)} %all-gather.3.cloned.1.call-done), slice={[0:2048], [0:512]} | slice | bytes 8388608 | tf_op jit(solution)/shard_map/split | solution.py:19
  206.7 72.9 %while.17 = (s32[]{:T(128)}, f32[4,512]{1,0:T(4,128)S(1)}, f32[4,256]{1,0:T(4,128)S(1)}, f32[4]{0:T(128)S(1)}, s32[4,512]{1,0:T(4,128)S(1)}, /*index=5*/f32[4,51...) while((s32[]{:T(128)}, f32[4,512]{1,0:T(4,128)S(1)}, ...), condition=%wide.region_5.6_spmd.clone, body=%wide.region_1.5_spmd.clone.sunk | while | flops 9673929728 | bytes 19969200 | solution.py:64
  206.7 1.4 fusion.33
  208.1 1.1 constant_dynamic-slice_fusion.4
  209.2 0.2 copy.9
  209.4 10.7 %fusion.35 = (f32[]{:T(128)}, f32[512,2048]{1,0:T(8,128)S(1)}) fusion(f32[2048,512]{1,0:T(8,128)} %get-tuple-element.322, f32[4,512,512]{2,1,0:T(8,128)} %get-tuple-element.320, s32[]{:T(128)S(6)} %copy.17, f32[2048]{0:T(1024)S(1)} %get-tuple-element.321, f32[512]{0:T(512)S(1)} %fusion.33, s32[2048]{0:T(1024)S(1)} %fusion.34, s32[512]{0:T(512)S(1)} %bitcast.46), kind=kOutput, calls=%fused_computation.33.clone.1 | convolution fusion | flops 6451888128 | bytes 9457672 | tf_op jit(solution)/shard_map/while/body/eval_jaxpr/dot_general | solution.py:41
  220.1 3.9 %fusion.36 = (f32[256]{0:T(256)S(1)}, f32[512,256]{0,1:T(8,128)S(1)}) fusion(f32[1,512,256]{1,2,0:T(8,128)S(1)} %copy.9, f32[512,2048]{1,0:T(8,128)S(1)} %get-tuple-element.285, f32[2048,256]{1,0:T(8,128)S(1)} %get-tuple-element.323), kind=kOutput, calls=%fused_computation.7.clone.1 | convolution fusion | flops 3221487360 | bytes 7341056 | tf_op jit(solution)/shard_map/while/body/eval_jaxpr/dot_general | solution.py:50
  224.1 0.8 dynamic_update_slice.26
  225.0 1.4 fusion.33
  226.4 1.1 constant_dynamic-slice_fusion.4
  227.4 0.2 copy.9
  227.6 10.7 %fusion.35 = (f32[]{:T(128)}, f32[512,2048]{1,0:T(8,128)S(1)}) fusion(f32[2048,512]{1,0:T(8,128)} %get-tuple-element.322, f32[4,512,512]{2,1,0:T(8,128)} %get-tuple-element.320, s32[]{:T(128)S(6)} %copy.17, f32[2048]{0:T(1024)S(1)} %get-tuple-element.321, f32[512]{0:T(512)S(1)} %fusion.33, s32[2048]{0:T(1024)S(1)} %fusion.34, s32[512]{0:T(512)S(1)} %bitcast.46), kind=kOutput, calls=%fused_computation.33.clone.1 | convolution fusion | flops 6451888128 | bytes 9457672 | tf_op jit(solution)/shard_map/while/body/eval_jaxpr/dot_general | solution.py:41
  238.4 3.9 %fusion.36 = (f32[256]{0:T(256)S(1)}, f32[512,256]{0,1:T(8,128)S(1)}) fusion(f32[1,512,256]{1,2,0:T(8,128)S(1)} %copy.9, f32[512,2048]{1,0:T(8,128)S(1)} %get-tuple-element.285, f32[2048,256]{1,0:T(8,128)S(1)} %get-tuple-element.323), kind=kOutput, calls=%fused_computation.7.clone.1 | convolution fusion | flops 3221487360 | bytes 7341056 | tf_op jit(solution)/shard_map/while/body/eval_jaxpr/dot_general | solution.py:50
  242.3 0.8 dynamic_update_slice.26
  243.2 1.4 fusion.33
  244.6 1.1 constant_dynamic-slice_fusion.4
  245.7 0.2 copy.9
  245.9 10.7 %fusion.35 = (f32[]{:T(128)}, f32[512,2048]{1,0:T(8,128)S(1)}) fusion(f32[2048,512]{1,0:T(8,128)} %get-tuple-element.322, f32[4,512,512]{2,1,0:T(8,128)} %get-tuple-element.320, s32[]{:T(128)S(6)} %copy.17, f32[2048]{0:T(1024)S(1)} %get-tuple-element.321, f32[512]{0:T(512)S(1)} %fusion.33, s32[2048]{0:T(1024)S(1)} %fusion.34, s32[512]{0:T(512)S(1)} %bitcast.46), kind=kOutput, calls=%fused_computation.33.clone.1 | convolution fusion | flops 6451888128 | bytes 9457672 | tf_op jit(solution)/shard_map/while/body/eval_jaxpr/dot_general | solution.py:41
  256.6 3.9 %fusion.36 = (f32[256]{0:T(256)S(1)}, f32[512,256]{0,1:T(8,128)S(1)}) fusion(f32[1,512,256]{1,2,0:T(8,128)S(1)} %copy.9, f32[512,2048]{1,0:T(8,128)S(1)} %get-tuple-element.285, f32[2048,256]{1,0:T(8,128)S(1)} %get-tuple-element.323), kind=kOutput, calls=%fused_computation.7.clone.1 | convolution fusion | flops 3221487360 | bytes 7341056 | tf_op jit(solution)/shard_map/while/body/eval_jaxpr/dot_general | solution.py:50
  260.6 0.8 dynamic_update_slice.26
  261.4 1.4 fusion.33
  262.8 1.1 constant_dynamic-slice_fusion.4
  263.9 0.2 copy.9
  264.1 10.7 %fusion.35 = (f32[]{:T(128)}, f32[512,2048]{1,0:T(8,128)S(1)}) fusion(f32[2048,512]{1,0:T(8,128)} %get-tuple-element.322, f32[4,512,512]{2,1,0:T(8,128)} %get-tuple-element.320, s32[]{:T(128)S(6)} %copy.17, f32[2048]{0:T(1024)S(1)} %get-tuple-element.321, f32[512]{0:T(512)S(1)} %fusion.33, s32[2048]{0:T(1024)S(1)} %fusion.34, s32[512]{0:T(512)S(1)} %bitcast.46), kind=kOutput, calls=%fused_computation.33.clone.1 | convolution fusion | flops 6451888128 | bytes 9457672 | tf_op jit(solution)/shard_map/while/body/eval_jaxpr/dot_general | solution.py:41
  274.9 3.9 %fusion.36 = (f32[256]{0:T(256)S(1)}, f32[512,256]{0,1:T(8,128)S(1)}) fusion(f32[1,512,256]{1,2,0:T(8,128)S(1)} %copy.9, f32[512,2048]{1,0:T(8,128)S(1)} %get-tuple-element.285, f32[2048,256]{1,0:T(8,128)S(1)} %get-tuple-element.323), kind=kOutput, calls=%fused_computation.7.clone.1 | convolution fusion | flops 3221487360 | bytes 7341056 | tf_op jit(solution)/shard_map/while/body/eval_jaxpr/dot_general | solution.py:50
  278.8 0.8 dynamic_update_slice.26
  279.7 0.6 reduce_sum.81
  280.3 7.6 %all-reduce.2 = (f32[256]{0:T(256)S(1)}, f32[]{:T(128)}) all-reduce(f32[256]{0:T(256)S(1)} %reduce_sum.82, f32[]{:T(128)} %reduce_sum.81), channel_id=1, replica_groups=mesh['row_0'=4,'row_1'=4,'col_0'=2,'col_1'=4,'col_2'=2] {'row_0'}, use_global_device_ids=true, to_apply=%region_13.14 | all-reduce | flops 257 | bytes 2056 | tf_op jit(solution)/shard_map/psum | solution.py:35
  287.9 9.0 %all-reduce.1 = (f32[256]{0:T(256)S(1)}, f32[]{:T(128)}) all-reduce(f32[256]{0:T(256)S(1)} %get-tuple-element.202, f32[]{:T(128)} %get-tuple-element.203), channel_id=1, replica_groups=mesh['row_0'=4,'row_1'=4,'col_0'=2,'col_1'=4,'col_2'=2] {'row_1'}, use_global_device_ids=true, to_apply=%region_14.15 | all-reduce | flops 257 | bytes 2056 | tf_op jit(solution)/shard_map/psum | solution.py:35
  296.9 8.3 %all-reduce.4 = (f32[256]{0:T(256)S(1)}, f32[]{:T(128)}) all-reduce(f32[256]{0:T(256)S(1)} %get-tuple-element.200, f32[]{:T(128)} %get-tuple-element.201), channel_id=1, replica_groups=mesh['row_0'=4,'row_1'=4,'col_0'=2,'col_1'=4,'col_2'=2] {'col_0'}, use_global_device_ids=true, to_apply=%region_15.16 | all-reduce | flops 257 | bytes 2056 | tf_op jit(solution)/shard_map/psum | solution.py:35
  305.2 8.4 %all-reduce = (f32[256]{0:T(256)S(1)}, f32[]{:T(128)}) all-reduce(f32[256]{0:T(256)S(1)} %get-tuple-element.206, f32[]{:T(128)} %get-tuple-element.207), channel_id=1, replica_groups=mesh['row_0'=4,'row_1'=4,'col_0'=2,'col_1'=4,'col_2'=2] {'col_1'}, use_global_device_ids=true, to_apply=%region_16.17 | all-reduce | flops 257 | bytes 2056 | tf_op jit(solution)/shard_map/psum | solution.py:35
  313.6 10.2 %all-reduce.3 = (f32[256]{0:T(256)S(1)}, f32[]{:T(128)}) all-reduce(f32[256]{0:T(256)S(1)} %get-tuple-element.198, f32[]{:T(128)} %get-tuple-element.199), channel_id=1, replica_groups=mesh['row_0'=4,'row_1'=4,'col_0'=2,'col_1'=4,'col_2'=2] {'col_2'}, use_global_device_ids=true, to_apply=%region_17.18 | all-reduce | flops 257 | bytes 2056 | tf_op jit(solution)/shard_map/psum | solution.py:35
  324.5 0.5 slice.12
  325.0 0.6 all_to_all.6
  325.6 3.6 %all-to-all-start = ((f32[16,1,128]{2,1,0:T(1,128)}), f32[16,1,128]{2,1,0:T(1,128)S(1)}, u32[]{:S(2)}, u32[]{:S(2)}) async-start(f32[16,1,128]{2,1,0:T(1,128)} %all_to_all.6), calls=%async_computation | async-start | bytes 16384 | tf_op jit(solution)/shard_map/all_to_all | solution.py:30
  329.3 1.3 fusion.17
  331.3 7.5 %all-to-all-done = f32[16,1,128]{2,1,0:T(1,128)S(1)} async-done(((f32[16,1,128]{2,1,0:T(1,128)}), f32[16,1,128]{2,1,0:T(1,128)S(1)}, u32[]{:S(2)}, u32[]{:S(2)}) %all-to-all-start) | async-done | bytes 8224 | tf_op jit(solution)/shard_map/all_to_all | solution.py:30
  338.8 0.5 broadcast_multiply_fusion
  (31 shorter events, 0.4 us)
Async XLA Ops:
  7.2 89.9 %all-gather.5.cloned.1.call-start = ((), (), s32[]{:S(2)}) async-start(), calls=%async_computation.2 | async-start | bytes 6684672 | tf_op jit(solution)/shard_map/all_gather | solution.py:18
  9.9 189.1 %all-gather.3.cloned.1.call-start = ((), (), s32[]{:S(2)}) async-start(), calls=%async_computation.1 | async-start | bytes 6684672 | tf_op jit(solution)/shard_map/all_gather | solution.py:18
  202.0 4.7 %slice-start = ((f32[2048,768]{1,0:T(8,128)}), f32[2048,256]{1,0:T(8,128)S(1)}, s32[]{:S(2)}) async-start(f32[2048,768]{1,0:T(8,128)} %all-gather.5.cloned.1.call-done), calls=%async_computation.3 | async-start | bytes 4194304 | tf_op jit(solution)/shard_map/split | solution.py:19
  324.5 14.8 %copy-start = (f32[256]{0:T(256)}, f32[256]{0:T(256)S(1)}, u32[]{:S(2)}) copy-start(f32[256]{0:T(256)S(1)} %multiply_add_fusion) | copy-start | bytes 3076
  325.6 13.1 %all-to-all-start = ((f32[16,1,128]{2,1,0:T(1,128)}), f32[16,1,128]{2,1,0:T(1,128)S(1)}, u32[]{:S(2)}, u32[]{:S(2)}) async-start(f32[16,1,128]{2,1,0:T(1,128)} %all_to_all.6), calls=%async_computation | async-start | bytes 16384 | tf_op jit(solution)/shard_map/all_to_all | solution.py:30
Sparse Core Ops, SparseCore 0:
  10.0 87.0 all-gather.4
  99.8 99.1 all-gather.2
where the time goes:
time: 348 us; the launch traced here: 347 us
  waiting for transfers between devices  192 us (55%)
  matrix products  58.7 us (17%)
  blocking collectives  43.6 us (13%)
  local copies, waits for them, and re-layouts  17.4 us (5%)
  between operations  16.6 us (5%)
  other arithmetic  15.2 us (4%)
  starting transfers between devices  3.71 us (1%)
    all_gather x2, waiting for transfers between devices, side_by_side(): out = lax.all_gather(both, axis, axis=dim, tiled=True)  184 us
    psum x5, blocking collectives, one_axis_at_a_time(): return functools.reduce(lax.psum, axes, shard)  43.6 us
    dot_general x4, matrix products, tile_terms(): lax.dot_general(xr, xc, (((1,), (1,)), ((), ())), precision=lax.Precision...  42.9 us
    dot_general x4, matrix products, tile_terms(): jnp.dot(kern, lc, precision=lax.Precision.HIGHEST, preferred_element_type...  15.8 us
    split x4, local copies, waits for them, and re-layouts, side_by_side(): jnp.split(out, [sum(widths[:k]) for k in range(1, len(widths))], axis=along)  7.76 us
    all_to_all x1, waiting for transfers between devices, summed_on_arrival(): lax.all_to_all(cut_along(shard, dim, length), axis, 0, 0, tiled=True)  7.51 us
  transfers between devices with their start and end apart: 3, of which 3 were waited for; matrix products, arithmetic and copies ran while one was open for 2% of the time, Pallas kernels for 0%

commit v1 on v0

v1 whole, which is shorter than its diff:
```python
import functools

import jax
import jax.numpy as jnp
from jax import lax
from jax.experimental import pallas as pl
from jax.experimental.pallas import tpu as pltpu
from jax.sharding import Mesh
from jax.sharding import PartitionSpec as P

AXES = ("zl", "x", "zh", "y", "c")
SIZES = (4, 4, 2, 4, 2)
BLK = 128
W = 512
PERMS = 256
COLS = W + PERMS
F32 = jnp.float32
BF16 = jnp.bfloat16

SELF = ((0, 0), (2, 0), (0, 2), (2, 2))
FULL = ((1, 0), (0, 3), (1, 1), (1, 3), (3, 2), (2, 1))


def index(zl, x, zh, y, c):
    return (((zl * 4 + x) * 2 + zh) * 4 + y) * 2 + c


def pairs(dx, dy, dz, dc):
    out = []
    for zl in range(4):
        for x in range(4):
            for zh in range(2):
                for y in range(4):
                    for c in range(2):
                        z = (zh * 4 + zl + dz) % 8
                        src = index(z % 4, (x + dx) % 4, z // 4, (y + dy) % 4, (c + dc) % 2)
                        out.append((src, index(zl, x, zh, y, c)))
    return out


def take(v, name, dx=0, dy=0, dz=0, dc=0):
    with jax.named_scope(name):
        return lax.ppermute(v, AXES, pairs(dx, dy, dz, dc))


def pack_kernel(s_ref, l_ref, o_ref):
    o_ref[:, :W] = s_ref[...]
    o_ref[:, W:] = l_ref[...].astype(F32)


def halves(x):
    hi = x.astype(BF16)
    return hi, (x - hi.astype(F32)).astype(BF16)


def spread_norm(x):
    n = jnp.sum(x * x, axis=1, keepdims=True) * (0.5 / W)
    return jnp.broadcast_to(n, (BLK, 128))


def pair_kernel(tiles, chunks, n_r, n_c, *refs):
    r_refs = refs[:n_r]
    c_refs = refs[n_r : n_r + n_c]
    out = refs[n_r + n_c]
    rs, cs, lc, ar, lr, bc, acc, wc, tt = refs[n_r + n_c + 1 :]
    for j, ref in enumerate(c_refs):
        x = ref[:, :W]
        hi, lo = halves(x)
        rows = slice(j * BLK, (j + 1) * BLK)
        cs[rows, :W] = hi
        cs[rows, W : 2 * W] = lo
        cs[rows, 2 * W :] = hi
        lc[rows, :] = ref[:, W:].astype(BF16)
        bc[:, rows] = spread_norm(x).T[:8, :]
    for i, ref in enumerate(r_refs):
        x = ref[:, :W]
        hi, lo = halves(x * (1.0 / W))
        rows = slice(i * BLK, (i + 1) * BLK)
        rs[rows, :W] = hi
        rs[rows, W : 2 * W] = hi
        rs[rows, 2 * W :] = lo
        ar[rows, :] = spread_norm(x)
        lr[rows, :] = jnp.broadcast_to(ref[:, W : W + 1], (BLK, 128))
    acc[...] = jnp.zeros_like(acc)
    wc[...] = jnp.zeros_like(wc)
    tt[...] = jnp.zeros_like(tt)

    def piece(t, start, width, weight, diag):
        rows = pl.ds(t * 256, 256) if isinstance(t, int) else pl.ds(pl.multiple_of(t * 256, 256), 256)
        cols = slice(start, start + width)
        s = lax.dot_general(rs[rows, :], cs[cols, :], (((1,), (1,)), ((), ())), preferred_element_type=F32)
        a = ar[rows, :]
        lrow = lr[rows, :]
        if width > 128:
            a = jnp.concatenate([a] * (width // 128), axis=1)
            lrow = jnp.concatenate([lrow] * (width // 128), axis=1)
        k = jnp.exp(jnp.minimum((s - a) - bc[0:1, cols], 0.0))
        if weight != 1.0:
            k = k * weight
        if diag:
            i = lax.broadcasted_iota(jnp.int32, k.shape, 0)
            j = lax.broadcasted_iota(jnp.int32, k.shape, 1)
            k = jnp.where((i == j) & (i < BLK), 0.0, k)
        hi, lo = halves(k)
        lab = lc[cols, :]
        acc[rows, :] += jnp.dot(hi, lab, preferred_element_type=F32) + jnp.dot(lo, lab, preferred_element_type=F32)
        wc[0:1, cols] += jnp.sum(k * lrow, axis=0, keepdims=True)
        tt[0:1, cols] += jnp.sum(k, axis=0, keepdims=True)

    start = 0
    for blocks, kind in chunks:
        width = blocks * BLK
        if kind == "full":

            def body(t, carry, start=start, width=width):
                piece(t, start, width, 1.0, False)
                return carry

            lax.fori_loop(0, len(tiles), body, 0)
        else:
            for t, dz in enumerate(tiles):
                if dz in (0, 4):
                    piece(t, start, width, 0.5, dz == 0 and kind == "own")
                elif dz < 4:
                    piece(t, start, width, 1.0, False)
        start += width

    quad = jnp.zeros((1, PERMS), F32)
    for i, ref in enumerate(r_refs):
        rows = slice(i * BLK, (i + 1) * BLK)
        part = acc[rows, :]
        quad = quad + jnp.sum(part * ref[:, W:], axis=0, keepdims=True)
        out[i : i + 1, :] = part[:, :128].T[0:1, :]
    tot = jnp.zeros((1, 128), F32)
    for j in range(n_c):
        cols = slice(j * BLK, (j + 1) * BLK)
        out[n_r + j : n_r + j + 1, :] = wc[0:1, cols]
        tot = tot + tt[0:1, cols]
    out[n_r + n_c : n_r + n_c + 1, :] = quad[:, :128]
    out[n_r + n_c + 1 : n_r + n_c + 2, :] = quad[:, 128:]
    out[n_r + n_c + 2 : n_r + n_c + 3, :] = tot


def pair_call(rows, columns, name):
    tiles = [dz for dz, _, _ in rows]
    r_in = [b for _, own, other in rows for b in (own, other)]
    chunks = [(len(blocks), kind) for blocks, kind in columns]
    c_in = [b for blocks, _ in columns for b in blocks]
    n_r, n_c = len(r_in), len(c_in)
    n_out = -(-(n_r + n_c + 3) // 8) * 8
    cells = sum(
        256 * b * BLK * (len(tiles) if kind == "full" else sum(dz <= 4 for dz in tiles)) for b, kind in chunks
    )
    vmem = pl.BlockSpec(memory_space=pltpu.VMEM)
    out = pl.pallas_call(
        functools.partial(pair_kernel, tiles, chunks, n_r, n_c),
        out_shape=jax.ShapeDtypeStruct((n_out, 128), F32),
        in_specs=[vmem] * (n_r + n_c),
        out_specs=vmem,
        scratch_shapes=[
            pltpu.VMEM((n_r * BLK, 3 * W), BF16),
            pltpu.VMEM((n_c * BLK, 3 * W), BF16),
            pltpu.VMEM((n_c * BLK, PERMS), BF16),
            pltpu.VMEM((n_r * BLK, 128), F32),
            pltpu.VMEM((n_r * BLK, 128), F32),
            pltpu.VMEM((8, n_c * BLK), F32),
            pltpu.VMEM((n_r * BLK, PERMS), F32),
            pltpu.VMEM((8, n_c * BLK), F32),
            pltpu.VMEM((8, n_c * BLK), F32),
        ],
        cost_estimate=pl.CostEstimate(
            flops=cells * 2 * (3 * W + 2 * PERMS), bytes_accessed=(n_r + n_c) * BLK * COLS * 4, transcendentals=cells
        ),
        name=name,
    )(*r_in, *c_in)
    return out[:n_r], out[n_r : n_r + n_c], out[n_r + n_c : n_r + n_c + 2].reshape(PERMS), out[n_r + n_c + 2]


def shards(samples, labels):
    vmem = pl.BlockSpec(memory_space=pltpu.VMEM)
    own = pl.pallas_call(
        pack_kernel,
        out_shape=jax.ShapeDtypeStruct((BLK, COLS), F32),
        in_specs=[vmem, vmem],
        out_specs=vmem,
        name="pack",
    )(samples, labels)
    c02 = take(own, "c02", dy=2)
    c20 = take(own, "c20", dx=2)
    u1 = take(own, "u1", dz=1)
    d1 = take(own, "d1", dz=-1)
    c10 = take(own, "c10", dx=1)
    c03 = take(own, "c03", dy=-1)
    o0 = take(own, "o0", dc=1)
    u2 = take(u1, "u2", dz=1)
    d2 = take(d1, "d2", dz=-1)
    c21 = take(c20, "c21", dy=1)
    c22 = take(c02, "c22", dx=2)
    c32 = take(c02, "c32", dx=-1)
    c11 = take(c10, "c11", dy=1)
    c13 = take(c10, "c13", dy=-1)
    u3 = take(u2, "u3", dz=1)
    d3 = take(d2, "d3", dz=-1)
    u4 = take(u3, "u4", dz=1)
    near = [(dz, b, take(b, f"o{dz}", dc=1)) for dz, b in ((1, u1), (7, d1), (2, u2), (6, d2))]
    mid = [(dz, b, take(b, f"o{dz}", dc=1)) for dz, b in ((3, u3), (5, d3))]
    last = [(4, u4, take(u4, "o4", dc=1))]
    near = [(0, own, o0)] + near
    first = [([c10, c03], "full"), ([own, c20], "own"), ([c02], "self")]
    second = [([c11, c13], "full"), ([c32, c21], "full"), ([c22], "self")]
    first_at = [(1, 0), (0, 3), (0, 0), (2, 0), (0, 2)]
    second_at = [(1, 1), (1, 3), (3, 2), (2, 1), (2, 2)]

    at = {a: lax.axis_index(a) for a in AXES}
    z = at["zh"] * 4 + at["zl"]
    peer = jnp.arange(256, dtype=jnp.int32)
    peer_c, peer_y, peer_x = peer % 2, peer // 2 % 4, peer // 16 % 4
    peer_z = peer // 8 % 2 * 4 + peer // 64

    def place(rows, here):
        return jnp.where(here[:, None], rows[None, :], 0.0)

    wit = jnp.zeros((256, BLK), F32)
    quad = jnp.zeros((PERMS,), F32)
    total = jnp.zeros((BLK,), F32)
    row_sums, col_sums = {}, {}
    for rows, columns, where, name in (
        (near, first, first_at, "near_first"),
        (near, second, second_at, "near_second"),
        (mid, first + second, first_at + second_at, "mid_all"),
        (last, first + second, first_at + second_at, "last_all"),
    ):
        r, c, q, t = pair_call(rows, columns, name)
        quad = quad + q
        total = total + t
        for i, (dz, _, _) in enumerate(rows):
            for side in range(2):
                key = (dz, side)
                row_sums[key] = row_sums.get(key, 0.0) + r[2 * i + side]
        for j, key in enumerate(where):
            col_sums[key] = col_sums.get(key, 0.0) + c[j]
    line = (peer_x == at["x"]) & (peer_y == at["y"])
    for (dz, side), v in row_sums.items():
        wit = wit + place(v, line & (peer_z == (z + dz) % 8) & (peer_c == (at["c"] + side) % 2))
    plane = (peer_z == z) & (peer_c == at["c"])
    for (dx, dy), v in col_sums.items():
        wit = wit + place(v, plane & (peer_x == (at["x"] + dx) % 4) & (peer_y == (at["y"] + dy) % 4))

    all_rows = samples.shape[0] * 256
    half = all_rows / 2.0
    share = 2.0 * jnp.sum(total) / (2.0 * half * (half - 1.0)) + (2.0 * half - 1.0) / (2.0 * half * (half - 1.0)) * (
        2.0 * quad
    )
    sent = jnp.concatenate([wit, jnp.broadcast_to(share[None, :], (256, PERMS))], axis=1)
    with jax.named_scope("meet"):
        got = jnp.sum(lax.all_to_all(sent, AXES, 0, 0, tiled=True), axis=0)
    proof = got[:BLK] / jnp.sqrt(jnp.float32(all_rows))
    statistic = got[BLK:]
    p_value = jnp.mean(jax.nn.sigmoid(4.0 * (statistic[1:] - statistic[0])))
    return (statistic, proof, p_value)


def solution(mesh):
    torus = Mesh(mesh.devices.reshape(SIZES), AXES)
    return jax.shard_map(
        shards,
        mesh=torus,
        in_specs=(P(AXES, None), P(AXES, None)),
        out_specs=(P(), P(AXES), P()),
        check_vma=False,
    )
```

time: 348 us -> 145 us (0.42)
  waiting for transfers between devices: 192 us -> 13.8 us
  matrix products: 58.7 us -> 0 us
  starting transfers between devices: 3.71 us -> 49.7 us
  Pallas kernels: 0 us -> 42.7 us
  blocking collectives: 43.6 us -> 25.3 us
  local copies, waits for them, and re-layouts: 17.4 us -> 2.92 us
  between operations: 16.6 us -> 3.3 us
  other arithmetic: 15.2 us -> 7.28 us
    all_gather x2 -> x0, waiting for transfers between devices: 184 us -> none  [side_by_side(): out = lax.all_gather(both, axis, axis=dim, tiled=True)]
    dot_general x8 -> x0, matrix products: 58.7 us -> none  [the longest x4 42.9 us: tile_terms(): lax.dot_general(xr, xc, (((1,), (1,)), ((), ())), precision=lax.Precision...]
    ppermute x0 -> x24, starting transfers between devices: none -> 49.7 us  [take(): return lax.ppermute(v, AXES, pairs(dx, dy, dz, dc))]
    psum x5 -> x0, blocking collectives: 43.6 us -> none  [one_axis_at_a_time(): return functools.reduce(lax.psum, axes, shard)]
    pallas_call x0 -> x5, Pallas kernels: none -> 42.7 us  [the longest x4 41 us: pair_call(): pl.pallas_call(functools.partial(pair_kernel, tiles, chunks, n_r, n_c), o...]
    all_to_all x0 -> x1, blocking collectives: none -> 25.3 us  [shards(): got = jnp.sum(lax.all_to_all(sent, AXES, 0, 0, tiled=True), axis=0)]
    ppermute x0 -> x24, waiting for transfers between devices: none -> 13.8 us  [take(): return lax.ppermute(v, AXES, pairs(dx, dy, dz, dc))]
    split x4 -> x0, local copies, waits for them, and re-layouts: 7.76 us -> none  [side_by_side(): jnp.split(out, [sum(widths[:k]) for k in range(1, len(widths))], axis=along)]
  transfers between devices with their start and end apart: 3 -> 24, of which waited for: 3 -> 5; matrix products, arithmetic and copies ran while one was open for 2% -> 1% of each run, Pallas kernels for 0% -> 24%
where the time goes in v1:
time: 145 us
  starting transfers between devices  49.7 us (34%)
  Pallas kernels  42.7 us (29%)
  blocking collectives  25.3 us (17%)
  waiting for transfers between devices  13.8 us (10%)
  other arithmetic  7.28 us (5%)
  between operations  3.3 us (2%)
  local copies, waits for them, and re-layouts  2.92 us (2%)
    ppermute x24, starting transfers between devices, take(): return lax.ppermute(v, AXES, pairs(dx, dy, dz, dc))  49.7 us
    pallas_call x4, Pallas kernels, pair_call(): pl.pallas_call(functools.partial(pair_kernel, tiles, chunks, n_r, n_c), o...  41 us
    all_to_all x1, blocking collectives, shards(): got = jnp.sum(lax.all_to_all(sent, AXES, 0, 0, tiled=True), axis=0)  25.3 us
    ppermute x24, waiting for transfers between devices, take(): return lax.ppermute(v, AXES, pairs(dx, dy, dz, dc))  13.8 us
  transfers between devices with their start and end apart: 24, of which 5 were waited for; matrix products, arithmetic and copies ran while one was open for 1% of the time, Pallas kernels for 24%

profile of v1, /device:TPU:1, one launch (start us, length us, event | category | flops | bytes accessed | tf_op | source)
XLA Modules:
  0.0 145.1 jit_solution(17341021781757123353)
XLA Ops:
  0.6 1.8 %pack.1.refs_0_.refs_12_.refs_6_.refs_4_ = f32[128,768]{1,0:T(8,128)} custom-call(f32[128,512]{1,0:T(8,128)} %s_ref.1, s32[128,256]{1,0:T(8,128)} %l_ref.1), custom_call_target="tpu_custom_call" | custom-call | tf_op jit(solution)/shard_map/pack/pallas_call | solution.py:181
  2.4 6.4 %collective-permute-start.1 = (f32[128,768]{1,0:T(8,128)}, f32[128,768]{1,0:T(8,128)S(1)}, u32[]{:S(2)}, u32[]{:S(2)}) collective-permute-start(f32[128,768]{1,0:T(8,128)} %pack.1.refs_0_.refs_12_.refs_6_.refs_4_), channel_id=1, source_target_pairs={{64,0},{65,1},{66,2},{67,3},{68,4},{69,5},{70,6},{71,7},{72,8},{73... | collective-permute-start | bytes 1179656 | tf_op jit(solution)/shard_map/u1/ppermute | solution.py:43
  8.8 2.5 %collective-permute-start.9 = (f32[128,768]{1,0:T(8,128)}, f32[128,768]{1,0:T(8,128)S(1)}, u32[]{:S(2)}, u32[]{:S(2)}) collective-permute-start(f32[128,768]{1,0:T(8,128)} %pack.1.refs_0_.refs_12_.refs_6_.refs_4_), channel_id=1, source_target_pairs={{16,0},{17,1},{18,2},{19,3},{20,4},{21,5},{22,6},{23,7},{24,8},{25... | collective-permute-start | bytes 1179656 | tf_op jit(solution)/shard_map/c10/ppermute | solution.py:43
  11.3 0.5 collective-permute-start.11
  11.8 2.9 %collective-permute-start.12 = (f32[128,768]{1,0:T(8,128)}, f32[128,768]{1,0:T(8,128)S(1)}, u32[]{:S(2)}, u32[]{:S(2)}) collective-permute-start(f32[128,768]{1,0:T(8,128)} %pack.1.refs_0_.refs_12_.refs_6_.refs_4_), channel_id=1, source_target_pairs={{4,0},{5,1},{6,2},{7,3},{0,4},{1,5},{2,6},{3,7},{12,8},{13,9},{14,... | collective-permute-start | bytes 1179656 | tf_op jit(solution)/shard_map/c02/ppermute | solution.py:43
  14.7 2.2 %collective-permute-done.1.refs_2_ = f32[128,768]{1,0:T(8,128)S(1)} collective-permute-done((f32[128,768]{1,0:T(8,128)}, f32[128,768]{1,0:T(8,128)S(1)}, u32[]{:S(2)}, u32[]{:S(2)}) %collective-permute-start.1) | collective-permute-done | bytes 393248 | tf_op jit(solution)/shard_map/u1/ppermute | solution.py:43
  16.9 1.5 %collective-permute-start = (f32[128,768]{1,0:T(8,128)}, f32[128,768]{1,0:T(8,128)S(1)}, u32[]{:S(2)}, u32[]{:S(2)}) collective-permute-start(f32[128,768]{1,0:T(8,128)} %pack.1.refs_0_.refs_12_.refs_6_.refs_4_), channel_id=1, source_target_pairs={{1,0},{0,1},{3,2},{2,3},{5,4},{4,5},{7,6},{6,7},{9,8},{8,9},{11,10... | collective-permute-start | bytes 1179656 | tf_op jit(solution)/shard_map/o0/ppermute | solution.py:43
  18.4 1.5 %collective-permute-done.9.refs_10_.refs_4_.refs_2_ = f32[128,768]{1,0:T(8,128)S(1)} collective-permute-done((f32[128,768]{1,0:T(8,128)}, f32[128,768]{1,0:T(8,128)S(1)}, u32[]{:S(2)}, u32[]{:S(2)}) %collective-permute-start.9) | collective-permute-done | bytes 393248 | tf_op jit(solution)/shard_map/c10/ppermute | solution.py:43
  19.9 1.8 %collective-permute-start.5 = (f32[128,768]{1,0:T(8,128)S(1)}, f32[128,768]{1,0:T(8,128)S(1)}, u32[]{:S(2)}, u32[]{:S(2)}) collective-permute-start(f32[128,768]{1,0:T(8,128)S(1)} %collective-permute-done.1.refs_2_), channel_id=1, source_target_pairs={{64,0},{65,1},{66,2},{67,3},{68,4},{69,5},{70,6},{71,7},{72,8},{73... | collective-permute-start | bytes 1179656 | tf_op jit(solution)/shard_map/u2/ppermute | solution.py:43
  21.7 0.7 collective-permute-done.11.refs_13_.refs_7_.refs_5_
  22.4 2.7 %collective-permute-start.13 = (f32[128,768]{1,0:T(8,128)S(1)}, f32[128,768]{1,0:T(8,128)S(1)}, u32[]{:S(2)}, u32[]{:S(2)}) collective-permute-start(f32[128,768]{1,0:T(8,128)S(1)} %collective-permute-done.9.refs_10_.refs_4_.refs_2_), channel_id=1, source_target_pairs={{2,0},{3,1},{4,2},{5,3},{6,4},{7,5},{0,6},{1,7},{10,8},{11,9},{12,... | collective-permute-start | bytes 1179656 | tf_op jit(solution)/shard_map/c11/ppermute | solution.py:43
  25.2 0.0 collective-permute-done.3.refs_4_
  25.2 6.9 %collective-permute-start.15 = (f32[128,768]{1,0:T(8,128)S(1)}, f32[128,768]{1,0:T(8,128)S(1)}, u32[]{:S(2)}, u32[]{:S(2)}) collective-permute-start(f32[128,768]{1,0:T(8,128)S(1)} %collective-permute-done.12.refs_14_.refs_8_.refs_6_), channel_id=1, source_target_pairs={{48,0},{49,1},{50,2},{51,3},{52,4},{53,5},{54,6},{55,7},{56,8},{57... | collective-permute-start | bytes 1179656 | tf_op jit(solution)/shard_map/c32/ppermute | solution.py:43
  32.1 2.6 %collective-permute-start.16 = (f32[128,768]{1,0:T(8,128)S(1)}, f32[128,768]{1,0:T(8,128)}, u32[]{:S(2)}, u32[]{:S(2)}) collective-permute-start(f32[128,768]{1,0:T(8,128)S(1)} %collective-permute-done.11.refs_13_.refs_7_.refs_5_), channel_id=1, source_target_pairs={{2,0},{3,1},{4,2},{5,3},{6,4},{7,5},{0,6},{1,7},{10,8},{11,9},{12,... | collective-permute-start | bytes 1179656 | tf_op jit(solution)/shard_map/c21/ppermute | solution.py:43
  34.7 1.5 %collective-permute-start.17 = (f32[128,768]{1,0:T(8,128)S(1)}, f32[128,768]{1,0:T(8,128)}, u32[]{:S(2)}, u32[]{:S(2)}) collective-permute-start(f32[128,768]{1,0:T(8,128)S(1)} %collective-permute-done.12.refs_14_.refs_8_.refs_6_), channel_id=1, source_target_pairs={{32,0},{33,1},{34,2},{35,3},{36,4},{37,5},{38,6},{39,7},{40,8},{41... | collective-permute-start | bytes 1179656 | tf_op jit(solution)/shard_map/c22/ppermute | solution.py:43
  36.2 0.0 collective-permute-done.13.refs_10_.refs_9_.refs_7_
  36.2 0.0 collective-permute-done.14.refs_11_.refs_10_.refs_8_
  36.2 6.5 %collective-permute-start.2 = (f32[128,768]{1,0:T(8,128)S(1)}, f32[128,768]{1,0:T(8,128)}, u32[]{:S(2)}, u32[]{:S(2)}) collective-permute-start(f32[128,768]{1,0:T(8,128)S(1)} %collective-permute-done.1.refs_2_), channel_id=1, source_target_pairs={{1,0},{0,1},{3,2},{2,3},{5,4},{4,5},{7,6},{6,7},{9,8},{8,9},{11,10... | collective-permute-start | bytes 1179656 | tf_op jit(solution)/shard_map/o1/ppermute | solution.py:43
  42.7 4.1 %collective-permute-start.4 = (f32[128,768]{1,0:T(8,128)}, f32[128,768]{1,0:T(8,128)}, u32[]{:S(2)}, u32[]{:S(2)}) collective-permute-start(f32[128,768]{1,0:T(8,128)} %collective-permute-done.3.refs_4_), channel_id=1, source_target_pairs={{1,0},{0,1},{3,2},{2,3},{5,4},{4,5},{7,6},{6,7},{9,8},{8,9},{11,10... | collective-permute-start | bytes 1179656 | tf_op jit(solution)/shard_map/o7/ppermute | solution.py:43
  46.8 0.8 collective-permute-start.18
  47.6 4.6 %collective-permute-start.6 = (f32[128,768]{1,0:T(8,128)}, f32[128,768]{1,0:T(8,128)}, u32[]{:S(2)}, u32[]{:S(2)}) collective-permute-start(f32[128,768]{1,0:T(8,128)} %copy-done.12), channel_id=1, source_target_pairs={{1,0},{0,1},{3,2},{2,3},{5,4},{4,5},{7,6},{6,7},{9,8},{8,9},{11,10... | collective-permute-start | bytes 1179656 | tf_op jit(solution)/shard_map/o2/ppermute | solution.py:43
  52.2 0.0 collective-permute-start.20
  52.2 0.1 collective-permute-start.8
  52.4 0.7 collective-permute-start.10
  53.0 4.6 %collective-permute-done.18.refs_0_ = f32[128,768]{1,0:T(8,128)} collective-permute-done((f32[128,768]{1,0:T(8,128)}, f32[128,768]{1,0:T(8,128)}, u32[]{:S(2)}, u32[]{:S(2)}) %collective-permute-start.18) | collective-permute-done | bytes 393248 | tf_op jit(solution)/shard_map/u3/ppermute | solution.py:43
  57.6 1.9 %collective-permute-start.22 = (f32[128,768]{1,0:T(8,128)}, f32[128,768]{1,0:T(8,128)}, u32[]{:S(2)}, u32[]{:S(2)}) collective-permute-start(f32[128,768]{1,0:T(8,128)} %collective-permute-done.18.refs_0_), channel_id=1, source_target_pairs={{64,0},{65,1},{66,2},{67,3},{68,4},{69,5},{70,6},{71,7},{72,8},{73... | collective-permute-start | bytes 1179656 | tf_op jit(solution)/shard_map/u4/ppermute | solution.py:43
  59.5 4.8 %collective-permute-done.20.refs_2_ = f32[128,768]{1,0:T(8,128)} collective-permute-done((f32[128,768]{1,0:T(8,128)}, f32[128,768]{1,0:T(8,128)}, u32[]{:S(2)}, u32[]{:S(2)}) %collective-permute-start.20) | collective-permute-done | bytes 393248 | tf_op jit(solution)/shard_map/d3/ppermute | solution.py:43
  64.4 0.9 collective-permute-start.19
  65.3 0.0 collective-permute-start.21
  65.3 13.3 %near_second.1 = f32[24,128]{1,0:T(8,128)} custom-call(f32[128,768]{1,0:T(8,128)} %pack.1.refs_0_.refs_12_.refs_6_.refs_4_, f32[128,768]{1,0:T(8,128)} %copy-done.11, f32[128,768]{1,0:T(8,128)} %copy-done.9, f32[128,768]{1,0:T(8,128)} %collective-permute-done.2.refs_3_, f32[128,768]{1,0:T(8,128)} %collective-permute-done.3.refs_4_, ...), custom_call_target="tpu_custom_call" | custom-call | flops 3087007744 | bytes 5898240 | tf_op jit(solution)/shard_map/near_second/pallas_call | solution.py:155
  78.6 11.7 %near_first.1 = f32[24,128]{1,0:T(8,128)} custom-call(f32[128,768]{1,0:T(8,128)} %pack.1.refs_0_.refs_12_.refs_6_.refs_4_, f32[128,768]{1,0:T(8,128)} %copy-done.11, f32[128,768]{1,0:T(8,128)} %copy-done.9, f32[128,768]{1,0:T(8,128)} %collective-permute-done.2.refs_3_, f32[128,768]{1,0:T(8,128)} %collective-permute-done.3.refs_4_, ...), custom_call_target="tpu_custom_call" | custom-call | flops 2550136832 | bytes 5898240 | tf_op jit(solution)/shard_map/near_first/pallas_call | solution.py:155
  90.3 0.9 fusion.31
  91.3 0.8 collective-permute-start.23
  92.1 10.4 %mid_all.1 = f32[24,128]{1,0:T(8,128)} custom-call(f32[128,768]{1,0:T(8,128)} %collective-permute-done.18.refs_0_, f32[128,768]{1,0:T(8,128)} %collective-permute-done.19.refs_1_, f32[128,768]{1,0:T(8,128)} %collective-permute-done.20.refs_2_, f32[128,768]{1,0:T(8,128)} %collective-permute-done.21.refs_3_, f32[128,768]{1,0:T(8,128)} %copy-done.4, ...), custom_call_target="tpu_custom_call" | custom-call | flops 2147483648 | bytes 5505024 | tf_op jit(solution)/shard_map/mid_all/pallas_call | solution.py:155
  102.5 0.8 slice_bitcast_fusion.3
  103.2 0.8 copy-done.13
  104.0 5.6 %last_all.1 = f32[16,128]{1,0:T(8,128)} custom-call(f32[128,768]{1,0:T(8,128)} %collective-permute-done.22.refs_0_, f32[128,768]{1,0:T(8,128)} %copy-done.13, f32[128,768]{1,0:T(8,128)} %copy-done.4, f32[128,768]{1,0:T(8,128)} %collective-permute-done.10.refs_11_.refs_5_.refs_3_, f32[128,768]{1,0:T(8,128)} %pack.1.refs_0_.refs_12_.refs_6_.refs_4_, ...), custom_call_target="tpu_custom_call" | custom-call | flops 1342177280 | bytes 4718592 | tf_op jit(solution)/shard_map/last_all/pallas_call | solution.py:155
  109.6 1.5 %fusion.11 = (f32[]{:T(128)}, f32[128]{0:T(128)S(1)}, f32[128]{0:T(128)S(1)}, f32[128]{0:T(128)S(1)}, f32[128]{0:T(128)S(1)}, /*index=5*/f32[128]{0:T(128)S(1)}) fusion(f32[16,128]{1,0:T(8,128)} %last_all.1, f32[24,128]{1,0:T(8,128)S(1)} %copy-done.3, f32[24,128]{1,0:T(8,128)S(1)} %copy-done.2, f32[24,128]{1,0:T(8,128)} %near_first.1), kind=kLoop, calls=%fused_computation.55 | loop fusion | flops 1791 | bytes 12292 | tf_op jit(solution)/shard_map/reduce_sum | solution.py:251
  111.1 0.9 fusion.21
  112.6 0.7 fusion.9
  113.3 1.0 select_add_fusion
  114.3 0.3 all_to_all.6
  114.6 25.3 %all_to_all.9 = f32[256,1,384]{2,1,0:T(1,128)S(1)} all-to-all(f32[256,1,384]{2,1,0:T(1,128)S(1)} %all_to_all.6), channel_id=1, replica_groups=mesh['zl'=4,'x'=4,'zh'=2,'y'=4,'c'=2] {'zl','x','zh','y','c'}, dimensions={0} | all-to-all | bytes 786432 | tf_op jit(solution)/shard_map/meet/all_to_all | solution.py:256
  140.0 0.3 reduce_sum.28
  140.3 0.6 slice.334
  140.9 0.5 slice_multiply_fusion
  141.4 0.5 slice.337
  141.9 1.4 fusion.10
  (52 shorter events, 0.2 us)
Async XLA Ops:
  2.4 50.0 %copy-start = (f32[128,768]{1,0:T(8,128)S(1)}, f32[128,768]{1,0:T(8,128)}, u32[]{:S(2)}) copy-start(f32[128,768]{1,0:T(8,128)} %pack.1.refs_0_.refs_12_.refs_6_.refs_4_) | copy-start | bytes 1179652
  2.4 14.5 %collective-permute-start.1 = (f32[128,768]{1,0:T(8,128)}, f32[128,768]{1,0:T(8,128)S(1)}, u32[]{:S(2)}, u32[]{:S(2)}) collective-permute-start(f32[128,768]{1,0:T(8,128)} %pack.1.refs_0_.refs_12_.refs_6_.refs_4_), channel_id=1, source_target_pairs={{64,0},{65,1},{66,2},{67,3},{68,4},{69,5},{70,6},{71,7},{72,8},{73... | collective-permute-start | bytes 1179656 | tf_op jit(solution)/shard_map/u1/ppermute | solution.py:43
  8.8 11.1 %collective-permute-start.9 = (f32[128,768]{1,0:T(8,128)}, f32[128,768]{1,0:T(8,128)S(1)}, u32[]{:S(2)}, u32[]{:S(2)}) collective-permute-start(f32[128,768]{1,0:T(8,128)} %pack.1.refs_0_.refs_12_.refs_6_.refs_4_), channel_id=1, source_target_pairs={{16,0},{17,1},{18,2},{19,3},{20,4},{21,5},{22,6},{23,7},{24,8},{25... | collective-permute-start | bytes 1179656 | tf_op jit(solution)/shard_map/c10/ppermute | solution.py:43
  11.3 11.1 %collective-permute-start.11 = (f32[128,768]{1,0:T(8,128)}, f32[128,768]{1,0:T(8,128)S(1)}, u32[]{:S(2)}, u32[]{:S(2)}) collective-permute-start(f32[128,768]{1,0:T(8,128)} %pack.1.refs_0_.refs_12_.refs_6_.refs_4_), channel_id=1, source_target_pairs={{32,0},{33,1},{34,2},{35,3},{36,4},{37,5},{38,6},{39,7},{40,8},{41... | collective-permute-start | bytes 1179656 | tf_op jit(solution)/shard_map/c20/ppermute | solution.py:43
  11.8 13.4 %collective-permute-start.12 = (f32[128,768]{1,0:T(8,128)}, f32[128,768]{1,0:T(8,128)S(1)}, u32[]{:S(2)}, u32[]{:S(2)}) collective-permute-start(f32[128,768]{1,0:T(8,128)} %pack.1.refs_0_.refs_12_.refs_6_.refs_4_), channel_id=1, source_target_pairs={{4,0},{5,1},{6,2},{7,3},{0,4},{1,5},{2,6},{3,7},{12,8},{13,9},{14,... | collective-permute-start | bytes 1179656 | tf_op jit(solution)/shard_map/c02/ppermute | solution.py:43
  14.7 10.5 %collective-permute-start.3 = (f32[128,768]{1,0:T(8,128)}, f32[128,768]{1,0:T(8,128)}, u32[]{:S(2)}, u32[]{:S(2)}) collective-permute-start(f32[128,768]{1,0:T(8,128)} %pack.1.refs_0_.refs_12_.refs_6_.refs_4_), channel_id=1, source_target_pairs={{200,0},{201,1},{202,2},{203,3},{204,4},{205,5},{206,6},{207,7},{1... | collective-permute-start | bytes 1179656 | tf_op jit(solution)/shard_map/d1/ppermute | solution.py:43
  16.9 48.4 %copy-start.9 = (f32[128,768]{1,0:T(8,128)}, f32[128,768]{1,0:T(8,128)S(1)}, u32[]{:S(2)}) copy-start(f32[128,768]{1,0:T(8,128)S(1)} %collective-permute-done.1.refs_2_) | copy-start | bytes 1179652
  16.9 15.2 %collective-permute-start = (f32[128,768]{1,0:T(8,128)}, f32[128,768]{1,0:T(8,128)S(1)}, u32[]{:S(2)}, u32[]{:S(2)}) collective-permute-start(f32[128,768]{1,0:T(8,128)} %pack.1.refs_0_.refs_12_.refs_6_.refs_4_), channel_id=1, source_target_pairs={{1,0},{0,1},{3,2},{2,3},{5,4},{4,5},{7,6},{6,7},{9,8},{8,9},{11,10... | collective-permute-start | bytes 1179656 | tf_op jit(solution)/shard_map/o0/ppermute | solution.py:43
  19.9 58.7 %copy-start.4 = (f32[128,768]{1,0:T(8,128)}, f32[128,768]{1,0:T(8,128)S(1)}, u32[]{:S(2)}) copy-start(f32[128,768]{1,0:T(8,128)S(1)} %collective-permute-done.9.refs_10_.refs_4_.refs_2_) | copy-start | bytes 1179652
  19.9 14.8 %collective-permute-start.5 = (f32[128,768]{1,0:T(8,128)S(1)}, f32[128,768]{1,0:T(8,128)S(1)}, u32[]{:S(2)}, u32[]{:S(2)}) collective-permute-start(f32[128,768]{1,0:T(8,128)S(1)} %collective-permute-done.1.refs_2_), channel_id=1, source_target_pairs={{64,0},{65,1},{66,2},{67,3},{68,4},{69,5},{70,6},{71,7},{72,8},{73... | collective-permute-start | bytes 1179656 | tf_op jit(solution)/shard_map/u2/ppermute | solution.py:43
  22.4 56.2 %copy-start.5 = (f32[128,768]{1,0:T(8,128)}, f32[128,768]{1,0:T(8,128)S(1)}, u32[]{:S(2)}) copy-start(f32[128,768]{1,0:T(8,128)S(1)} %collective-permute-done.11.refs_13_.refs_7_.refs_5_) | copy-start | bytes 1179652
  22.4 13.8 %collective-permute-start.13 = (f32[128,768]{1,0:T(8,128)S(1)}, f32[128,768]{1,0:T(8,128)S(1)}, u32[]{:S(2)}, u32[]{:S(2)}) collective-permute-start(f32[128,768]{1,0:T(8,128)S(1)} %collective-permute-done.9.refs_10_.refs_4_.refs_2_), channel_id=1, source_target_pairs={{2,0},{3,1},{4,2},{5,3},{6,4},{7,5},{0,6},{1,7},{10,8},{11,9},{12,... | collective-permute-start | bytes 1179656 | tf_op jit(solution)/shard_map/c11/ppermute | solution.py:43
  25.2 53.5 %copy-start.6 = (f32[128,768]{1,0:T(8,128)}, f32[128,768]{1,0:T(8,128)S(1)}, u32[]{:S(2)}) copy-start(f32[128,768]{1,0:T(8,128)S(1)} %collective-permute-done.12.refs_14_.refs_8_.refs_6_) | copy-start | bytes 1179652
  25.2 11.1 %collective-permute-start.14 = (f32[128,768]{1,0:T(8,128)S(1)}, f32[128,768]{1,0:T(8,128)S(1)}, u32[]{:S(2)}, u32[]{:S(2)}) collective-permute-start(f32[128,768]{1,0:T(8,128)S(1)} %collective-permute-done.9.refs_10_.refs_4_.refs_2_), channel_id=1, source_target_pairs={{6,0},{7,1},{0,2},{1,3},{2,4},{3,5},{4,6},{5,7},{14,8},{15,9},{8,1... | collective-permute-start | bytes 1179656 | tf_op jit(solution)/shard_map/c13/ppermute | solution.py:43
  25.2 17.5 %collective-permute-start.15 = (f32[128,768]{1,0:T(8,128)S(1)}, f32[128,768]{1,0:T(8,128)S(1)}, u32[]{:S(2)}, u32[]{:S(2)}) collective-permute-start(f32[128,768]{1,0:T(8,128)S(1)} %collective-permute-done.12.refs_14_.refs_8_.refs_6_), channel_id=1, source_target_pairs={{48,0},{49,1},{50,2},{51,3},{52,4},{53,5},{54,6},{55,7},{56,8},{57... | collective-permute-start | bytes 1179656 | tf_op jit(solution)/shard_map/c32/ppermute | solution.py:43
  32.1 10.6 %copy-start.11 = (f32[128,768]{1,0:T(8,128)}, f32[128,768]{1,0:T(8,128)S(1)}, u32[]{:S(2)}) copy-start(f32[128,768]{1,0:T(8,128)S(1)} %collective-permute-done.refs_1_) | copy-start | bytes 1179652
  32.1 14.7 %collective-permute-start.16 = (f32[128,768]{1,0:T(8,128)S(1)}, f32[128,768]{1,0:T(8,128)}, u32[]{:S(2)}, u32[]{:S(2)}) collective-permute-start(f32[128,768]{1,0:T(8,128)S(1)} %collective-permute-done.11.refs_13_.refs_7_.refs_5_), channel_id=1, source_target_pairs={{2,0},{3,1},{4,2},{5,3},{6,4},{7,5},{0,6},{1,7},{10,8},{11,9},{12,... | collective-permute-start | bytes 1179656 | tf_op jit(solution)/shard_map/c21/ppermute | solution.py:43
  34.7 12.1 %copy-start.12 = (f32[128,768]{1,0:T(8,128)}, f32[128,768]{1,0:T(8,128)S(1)}, u32[]{:S(2)}) copy-start(f32[128,768]{1,0:T(8,128)S(1)} %collective-permute-done.5.refs_6_) | copy-start | bytes 1179652
  34.7 12.9 %collective-permute-start.17 = (f32[128,768]{1,0:T(8,128)S(1)}, f32[128,768]{1,0:T(8,128)}, u32[]{:S(2)}, u32[]{:S(2)}) collective-permute-start(f32[128,768]{1,0:T(8,128)S(1)} %collective-permute-done.12.refs_14_.refs_8_.refs_6_), channel_id=1, source_target_pairs={{32,0},{33,1},{34,2},{35,3},{36,4},{37,5},{38,6},{39,7},{40,8},{41... | collective-permute-start | bytes 1179656 | tf_op jit(solution)/shard_map/c22/ppermute | solution.py:43
  36.2 29.1 %copy-start.7 = (f32[128,768]{1,0:T(8,128)}, f32[128,768]{1,0:T(8,128)S(1)}, u32[]{:S(2)}) copy-start(f32[128,768]{1,0:T(8,128)S(1)} %collective-permute-done.13.refs_10_.refs_9_.refs_7_) | copy-start | bytes 1179652
  36.2 16.0 %collective-permute-start.7 = (f32[128,768]{1,0:T(8,128)}, f32[128,768]{1,0:T(8,128)}, u32[]{:S(2)}, u32[]{:S(2)}) collective-permute-start(f32[128,768]{1,0:T(8,128)} %collective-permute-done.3.refs_4_), channel_id=1, source_target_pairs={{200,0},{201,1},{202,2},{203,3},{204,4},{205,5},{206,6},{207,7},{1... | collective-permute-start | bytes 1179656 | tf_op jit(solution)/shard_map/d2/ppermute | solution.py:43
  36.2 29.1 %copy-start.8 = (f32[128,768]{1,0:T(8,128)}, f32[128,768]{1,0:T(8,128)S(1)}, u32[]{:S(2)}) copy-start(f32[128,768]{1,0:T(8,128)S(1)} %collective-permute-done.14.refs_11_.refs_10_.refs_8_) | copy-start | bytes 1179652
  36.2 16.0 %collective-permute-start.2 = (f32[128,768]{1,0:T(8,128)S(1)}, f32[128,768]{1,0:T(8,128)}, u32[]{:S(2)}, u32[]{:S(2)}) collective-permute-start(f32[128,768]{1,0:T(8,128)S(1)} %collective-permute-done.1.refs_2_), channel_id=1, source_target_pairs={{1,0},{0,1},{3,2},{2,3},{5,4},{4,5},{7,6},{6,7},{9,8},{8,9},{11,10... | collective-permute-start | bytes 1179656 | tf_op jit(solution)/shard_map/o1/ppermute | solution.py:43
  42.7 22.6 %copy-start.10 = (f32[128,768]{1,0:T(8,128)}, f32[128,768]{1,0:T(8,128)S(1)}, u32[]{:S(2)}) copy-start(f32[128,768]{1,0:T(8,128)S(1)} %collective-permute-done.15.refs_12_.refs_11_.refs_9_) | copy-start | bytes 1179652
  42.7 9.6 %collective-permute-start.4 = (f32[128,768]{1,0:T(8,128)}, f32[128,768]{1,0:T(8,128)}, u32[]{:S(2)}, u32[]{:S(2)}) collective-permute-start(f32[128,768]{1,0:T(8,128)} %collective-permute-done.3.refs_4_), channel_id=1, source_target_pairs={{1,0},{0,1},{3,2},{2,3},{5,4},{4,5},{7,6},{6,7},{9,8},{8,9},{11,10... | collective-permute-start | bytes 1179656 | tf_op jit(solution)/shard_map/o7/ppermute | solution.py:43
  46.8 10.8 %collective-permute-start.18 = (f32[128,768]{1,0:T(8,128)}, f32[128,768]{1,0:T(8,128)}, u32[]{:S(2)}, u32[]{:S(2)}) collective-permute-start(f32[128,768]{1,0:T(8,128)} %copy-done.12), channel_id=1, source_target_pairs={{64,0},{65,1},{66,2},{67,3},{68,4},{69,5},{70,6},{71,7},{72,8},{73... | collective-permute-start | bytes 1179656 | tf_op jit(solution)/shard_map/u3/ppermute | solution.py:43
  47.6 17.7 %collective-permute-start.6 = (f32[128,768]{1,0:T(8,128)}, f32[128,768]{1,0:T(8,128)}, u32[]{:S(2)}, u32[]{:S(2)}) collective-permute-start(f32[128,768]{1,0:T(8,128)} %copy-done.12), channel_id=1, source_target_pairs={{1,0},{0,1},{3,2},{2,3},{5,4},{4,5},{7,6},{6,7},{9,8},{8,9},{11,10... | collective-permute-start | bytes 1179656 | tf_op jit(solution)/shard_map/o2/ppermute | solution.py:43
  52.2 12.2 %collective-permute-start.20 = (f32[128,768]{1,0:T(8,128)}, f32[128,768]{1,0:T(8,128)}, u32[]{:S(2)}, u32[]{:S(2)}) collective-permute-start(f32[128,768]{1,0:T(8,128)} %collective-permute-done.7.refs_8_), channel_id=1, source_target_pairs={{200,0},{201,1},{202,2},{203,3},{204,4},{205,5},{206,6},{207,7},{1... | collective-permute-start | bytes 1179656 | tf_op jit(solution)/shard_map/d3/ppermute | solution.py:43
  52.2 13.1 %collective-permute-start.8 = (f32[128,768]{1,0:T(8,128)}, f32[128,768]{1,0:T(8,128)}, u32[]{:S(2)}, u32[]{:S(2)}) collective-permute-start(f32[128,768]{1,0:T(8,128)} %collective-permute-done.7.refs_8_), channel_id=1, source_target_pairs={{1,0},{0,1},{3,2},{2,3},{5,4},{4,5},{7,6},{6,7},{9,8},{8,9},{11,10... | collective-permute-start | bytes 1179656 | tf_op jit(solution)/shard_map/o6/ppermute | solution.py:43
  52.4 26.3 %collective-permute-start.10 = (f32[128,768]{1,0:T(8,128)S(1)}, f32[128,768]{1,0:T(8,128)}, u32[]{:S(2)}, u32[]{:S(2)}) collective-permute-start(f32[128,768]{1,0:T(8,128)S(1)} %copy-done), channel_id=1, source_target_pairs={{6,0},{7,1},{0,2},{1,3},{2,4},{3,5},{4,6},{5,7},{14,8},{15,9},{8,1... | collective-permute-start | bytes 1179656 | tf_op jit(solution)/shard_map/c03/ppermute | solution.py:43
  57.6 33.6 %collective-permute-start.22 = (f32[128,768]{1,0:T(8,128)}, f32[128,768]{1,0:T(8,128)}, u32[]{:S(2)}, u32[]{:S(2)}) collective-permute-start(f32[128,768]{1,0:T(8,128)} %collective-permute-done.18.refs_0_), channel_id=1, source_target_pairs={{64,0},{65,1},{66,2},{67,3},{68,4},{69,5},{70,6},{71,7},{72,8},{73... | collective-permute-start | bytes 1179656 | tf_op jit(solution)/shard_map/u4/ppermute | solution.py:43
  64.4 27.7 %collective-permute-start.19 = (f32[128,768]{1,0:T(8,128)}, f32[128,768]{1,0:T(8,128)}, u32[]{:S(2)}, u32[]{:S(2)}) collective-permute-start(f32[128,768]{1,0:T(8,128)} %collective-permute-done.18.refs_0_), channel_id=1, source_target_pairs={{1,0},{0,1},{3,2},{2,3},{5,4},{4,5},{7,6},{6,7},{9,8},{8,9},{11,10... | collective-permute-start | bytes 1179656 | tf_op jit(solution)/shard_map/o3/ppermute | solution.py:43
  65.3 26.8 %collective-permute-start.21 = (f32[128,768]{1,0:T(8,128)}, f32[128,768]{1,0:T(8,128)}, u32[]{:S(2)}, u32[]{:S(2)}) collective-permute-start(f32[128,768]{1,0:T(8,128)} %collective-permute-done.20.refs_2_), channel_id=1, source_target_pairs={{1,0},{0,1},{3,2},{2,3},{5,4},{4,5},{7,6},{6,7},{9,8},{8,9},{11,10... | collective-permute-start | bytes 1179656 | tf_op jit(solution)/shard_map/o5/ppermute | solution.py:43
  78.6 11.7 %copy-start.2 = (f32[24,128]{1,0:T(8,128)S(1)}, f32[24,128]{1,0:T(8,128)}, u32[]{:S(2)}) copy-start(f32[24,128]{1,0:T(8,128)} %near_second.1) | copy-start | bytes 36868
  91.3 12.0 %collective-permute-start.23 = (f32[128,768]{1,0:T(8,128)}, f32[128,768]{1,0:T(8,128)S(1)}, u32[]{:S(2)}, u32[]{:S(2)}) collective-permute-start(f32[128,768]{1,0:T(8,128)} %collective-permute-done.22.refs_0_), channel_id=1, source_target_pairs={{1,0},{0,1},{3,2},{2,3},{5,4},{4,5},{7,6},{6,7},{9,8},{8,9},{11,10... | collective-permute-start | bytes 1179656 | tf_op jit(solution)/shard_map/o4/ppermute | solution.py:43
  103.2 6.3 %copy-start.3 = (f32[24,128]{1,0:T(8,128)S(1)}, f32[24,128]{1,0:T(8,128)}, u32[]{:S(2)}) copy-start(f32[24,128]{1,0:T(8,128)} %mid_all.1) | copy-start | bytes 36868
  103.2 0.8 copy-start.13
  109.6 1.5 %copy-start.1 = (f32[16,128]{1,0:T(8,128)S(1)}, f32[16,128]{1,0:T(8,128)}, u32[]{:S(2)}) copy-start(f32[16,128]{1,0:T(8,128)} %last_all.1) | copy-start | bytes 24580
